TPU v7x, 256 devices: a whole 4x4x8 slice. The times are simulated.
256 devices in a mesh: px: 32 (over x, y, core), py: 8 (over z).
Axes of the slice: x: 4, y: 4, z: 8, core: 2. Of those that a mesh axis runs over, the one named last changes fastest.
Arguments:
- cell_ids: int32 [32, 5120, 128], P('px', 'py'), may hold values from 0 to 32767, as said below
- offset_x: bfloat16 [32, 5120, 128], P('px', 'py'), may hold values from 0 to 1
- offset_y: bfloat16 [32, 5120, 128], P('px', 'py'), may hold values from 0 to 1
- mass: bfloat16 [32, 5120, 128], P('px', 'py'), may hold values from 0.25 to 4
- live: int32 [32, 5120, 128], P('px', 'py'), may hold values from 0 to 1, as said below
- tile_owner: int32 [32, 5120], P('px', 'py'), may hold values from 0 to 31, as said below
- counts: int32 [32, 8, 256], P('px', 'py'), may hold values from 0 to 7680, as said below
Outputs:
- spectrum: float32 [2, 8, 1024, 1024], P(None, None, ('px', 'py'))
- bucket_start: int32 [32, 8, 256], P('px', 'py')
Inputs may be any that keep to these rules, and one draw needn't show every extreme that they name: A device's tiles stand in order of bucket, bucket = tile_owner * 8 + plane. One device has at most 60 tiles of one owner; in every draw, in each column of py, one owner has exactly 60 tiles on every device of that column. `cell_ids`: cell = (plane * 32 + row) * 128 + column, with row inside the owner's block of rows and column inside the device's block of columns; all slots of a tile, padded ones too, carry the tile's plane. In a tile the live particles come first; only the last tile of a bucket on a device has padded slots. counts[i, j, b] is the number of live particles in the tiles of bucket b on device (i, j); in every draw some bucket of every device holds 7680.
All inputs are finite; a program needn't handle non-finite values.
Results may differ from a plain program's by a relative error of at most 0.0003.
The roundings to bfloat16 on the way count: a program that leaves them out, or rounds other values in their place, can miss the bound.
Values may be sent and summed in bfloat16 or wider, within the bound.
A program may use at most 128 MiB of HBM per device.

v0:
```python
import functools
import math

import jax
import jax.numpy as jnp
import numpy as np
from jax import lax
from jax.experimental import pallas as pl
from jax.experimental.pallas import tpu as pltpu
from jax.sharding import Mesh
from jax.sharding import PartitionSpec as P

NX = 1024
NY = 1024
PLANES = 8
BETA = 18.4
OWNERS = 32
BLOCKS = OWNERS + 2
RX = 32
TILE = 128
NT = (((1,), (1,)), ((), ()))


def tap_values(step, fraction):
    z = (step.astype(jnp.float32) - fraction) * 0.25
    return jnp.exp(BETA * (jnp.sqrt(1.0 - z * z) - 1.0))


def spread_kernel(
    owner_hbm, cell_hbm, fx_hbm, fy_hbm, mass_hbm, live_hbm,
    main_ref, rim_ref, total_ref,
    owner_ref, cell_ref, fx_ref, fy_ref, mass_ref, live_ref, in_sem,
    rim_acc, lx_s, ly_s, fx_s, fy_s, w_s,
):
    tiles = cell_ref.shape[0]
    sources = (owner_hbm, cell_hbm, fx_hbm, fy_hbm, mass_hbm, live_hbm)
    homes = (owner_ref, cell_ref, fx_ref, fy_ref, mass_ref, live_ref)
    arrivals = [
        pltpu.make_async_copy(source, home, in_sem.at[k]) for k, (source, home) in enumerate(zip(sources, homes))
    ]
    for copy in arrivals:
        copy.start()
    zero = jnp.zeros((8, TILE), jnp.float32)

    def clear(i, _):
        for p in range(PLANES):
            for k in range(RX // 8):
                main_ref[i * PLANES + p, 8 * k : 8 * k + 8, :] = zero
        for k in range(RX // 8):
            rim_acc[i, 8 * k : 8 * k + 8, :] = zero
        return 0

    lax.fori_loop(0, BLOCKS, clear, 0)

    for copy in arrivals:
        copy.wait()

    def prepare(i, _):
        rows = pl.ds(pl.multiple_of(i * 16, 16), 16)
        cell = cell_ref[rows, :]
        ly_s[rows, :] = cell & 127
        lx_s[rows, :] = (cell >> 7) & 31
        fx_s[rows, :] = fx_ref[rows, :].astype(jnp.float32)
        fy_s[rows, :] = fy_ref[rows, :].astype(jnp.float32)
        w_s[rows, :] = jnp.where(live_ref[rows, :] == 1, mass_ref[rows, :].astype(jnp.float32), 0.0)
        return 0

    lax.fori_loop(0, tiles // 16, prepare, 0)

    sub = lax.broadcasted_iota(jnp.int32, (8, TILE), 0)

    def row(ref, t):
        return jnp.broadcast_to(ref[pl.ds(t, 1), :], (8, TILE))

    def one_tile(t):
        lx, ly = row(lx_s, t), row(ly_s, t)
        jx = (sub - lx + 3) & 7
        jy = (sub - ly + 3) & 7
        tx = tap_values(jx - 3, row(fx_s, t))
        ty = tap_values(jy - 3, row(fy_s, t)) * row(w_s, t)
        gx = (lx + jx + 5) >> 3
        gy = (ly + jy - 3) >> 3
        gy = jnp.where(gy < 0, 16, gy)
        wx = jnp.concatenate([jnp.where(gx == g, tx, 0.0) for g in range(6)]).astype(jnp.bfloat16)
        wy = jnp.concatenate([*(jnp.where(gy == g, ty, 0.0) for g in range(17)), zero]).astype(jnp.bfloat16)
        return lax.dot_general(wx, wy, NT, preferred_element_type=jnp.float32)

    blank = jnp.zeros((48, TILE - 8), jnp.float32)

    unroll = 320

    def add_tiles(i, _):
        results = [one_tile(i * unroll + k) for k in range(unroll)]
        for k in range(unroll):
            owner = owner_ref[0, i * unroll + k]
            plane = cell_ref[pl.ds(i * unroll + k, 1), :][0, 0] >> 12
            main, rim = results[k][:, :TILE], results[k][:, TILE : TILE + 8]
            rim = pltpu.roll(jnp.concatenate([rim, blank], axis=1), 8 * plane, 1)
            for blocks, spot, part in ((main_ref, plane * BLOCKS + owner, main), (rim_acc, owner, rim)):
                blocks[spot, 24:32, :] = blocks[spot, 24:32, :] + part[:8]
                blocks[spot + 1] = blocks[spot + 1] + part[8:40]
                blocks[spot + 2, 0:8, :] = blocks[spot + 2, 0:8, :] + part[40:]
        return 0

    lax.fori_loop(0, tiles // unroll, add_tiles, 0)

    for blocks, start in ((rim_acc, 0), *((main_ref, p * BLOCKS) for p in range(PLANES))):
        first, last = start, start + OWNERS
        blocks[last, 24:32, :] = blocks[last, 24:32, :] + blocks[first, 24:32, :]
        blocks[first + 1, 0:8, :] = blocks[first + 1, 0:8, :] + blocks[last + 1, 0:8, :]

    def write_out(i, total):
        parts = [main_ref[p * BLOCKS + i + 1, 8 * k : 8 * k + 8, :] for p in range(PLANES) for k in range(RX // 8)]
        while len(parts) > 1:
            parts = [one + two for one, two in zip(parts[::2], parts[1::2])]
        total = total + parts[0]
        for q in range(2):
            near_rows, far_rows = rim_acc[i + 1, 8 * q : 8 * q + 8, :], rim_acc[i + 1, 8 * q + 16 : 8 * q + 24, :]
            out = near_rows + pltpu.roll(far_rows, 64, 1)
            rim_ref[q, i // 2, i % 2] = out
            total = total + out
        return total

    total_ref[...] = lax.fori_loop(0, OWNERS, write_out, zero, unroll=8)


def spread(owners, cells, fx, fy, mass, live):
    tiles = cells.shape[0]
    vmem = pl.BlockSpec(memory_space=pltpu.VMEM)
    return pl.pallas_call(
        spread_kernel,
        out_shape=(
            jax.ShapeDtypeStruct((PLANES * BLOCKS, RX, TILE), jnp.float32),
            jax.ShapeDtypeStruct((2, 16, 2, 8, TILE), jnp.float32),
            jax.ShapeDtypeStruct((8, TILE), jnp.float32),
        ),
        in_specs=[pl.BlockSpec(memory_space=pltpu.HBM)] * 6,
        out_specs=(vmem, vmem, vmem),
        scratch_shapes=[
            pltpu.SMEM((1, tiles), jnp.int32),
            pltpu.VMEM((tiles, TILE), jnp.int32),
            pltpu.VMEM((tiles, TILE), jnp.bfloat16),
            pltpu.VMEM((tiles, TILE), jnp.bfloat16),
            pltpu.VMEM((tiles, TILE), jnp.bfloat16),
            pltpu.VMEM((tiles, TILE), jnp.int32),
            pltpu.SemaphoreType.DMA((6,)),
            pltpu.VMEM((BLOCKS, RX, TILE), jnp.float32),
            pltpu.VMEM((tiles, TILE), jnp.int32),
            pltpu.VMEM((tiles, TILE), jnp.int32),
            pltpu.VMEM((tiles, TILE), jnp.float32),
            pltpu.VMEM((tiles, TILE), jnp.float32),
            pltpu.VMEM((tiles, TILE), jnp.float32),
        ],
        compiler_params=pltpu.CompilerParams(vmem_limit_bytes=24 << 20),
        name="spread",
    )(*(pltpu.with_memory_space_constraint(a, pltpu.HBM) for a in (owners, cells, fx, fy, mass, live)))


COORDS = ("px_0", "px_1", "px_2")
DEVICES = 256


def split_bf16(value):
    high = value.astype(jnp.bfloat16)
    return high, (value - high.astype(jnp.float32)).astype(jnp.bfloat16)


def np_split(value):
    high = np.asarray(value, np.float32).astype(jnp.bfloat16)
    low = (np.asarray(value, np.float64) - high.astype(np.float64)).astype(jnp.bfloat16)
    return high, low


def tables():
    k = np.arange(TILE)
    turn_y = 2 * np.pi / NY * (np.arange(8)[:, None] * k[None, :])
    twist_y = np.stack([np.cos(turn_y), -np.sin(turn_y)]).astype(np.float32)
    theta = 2 * np.pi / TILE * (k[:, None] * k[None, :] % TILE)
    wave_y = np.zeros((TILE, 2, 2, TILE))
    wave_y[:, 0, 0], wave_y[:, 0, 1] = np.cos(theta), np.sin(theta)
    wave_y[:, 1, 0], wave_y[:, 1, 1] = -np.sin(theta), np.cos(theta)
    y_high, y_low = np_split(wave_y.reshape(2 * TILE, 2 * TILE))
    phase = 2 * np.pi / OWNERS * (np.arange(OWNERS)[:, None] * k[None, :] % OWNERS)
    block = np.zeros((OWNERS, 2, 2, TILE))
    block[:, 0, 0], block[:, 1, 0] = np.cos(phase), np.sin(phase)
    block[:, 0, 1], block[:, 1, 1] = -np.sin(phase), np.cos(phase)
    wave_x = np.kron(np.eye(2), block.reshape(2 * OWNERS, 2 * TILE))
    x_high, x_low = np_split(wave_x)
    turn_x = 2 * np.pi / NX * (np.arange(RX)[:, None] * k[None, :])
    scale = 1.0 / math.sqrt(NX * NY)
    twist_x = (scale * np.stack([np.cos(turn_x), -np.sin(turn_x)])).astype(np.float32)
    return (twist_y, y_high, y_low), (np.concatenate([x_high, x_high]), x_low, twist_x)


HALF = math.sqrt(0.5)


def real_eighths(d):
    s = [d[k] + d[k + 4] for k in range(4)]
    e = [d[k] - d[k + 4] for k in range(4)]
    near_sum, far_sum = s[0] + s[2], s[1] + s[3]
    a0, a4 = near_sum + far_sum, near_sum - far_sum
    re2, im2 = s[0] - s[2], s[3] - s[1]
    tilt, lean = (e[1] - e[3]) * HALF, (e[1] + e[3]) * HALF
    re1, im1 = e[0] + tilt, -e[2] - lean
    re3, im3 = e[0] - tilt, e[2] - lean
    zero = jnp.zeros_like(a0)
    return [(a0, zero), (re1, im1), (re2, im2), (re3, im3), (a4, zero), (re3, -im3), (re2, -im2), (re1, -im1)]


def fourths(t):
    def add(p, q):
        return p[0] + q[0], p[1] + q[1]

    def less(p, q):
        return p[0] - q[0], p[1] - q[1]

    e0, e1 = add(t[0], t[2]), less(t[0], t[2])
    f0, g = add(t[1], t[3]), less(t[1], t[3])
    f1 = (g[1], -g[0])
    return [add(e0, f0), add(e1, f1), less(e0, f0), less(e1, f1)]


def eighths(z):
    s = [(z[k][0] + z[k + 4][0], z[k][1] + z[k + 4][1]) for k in range(4)]
    d = [(z[k][0] - z[k + 4][0], z[k][1] - z[k + 4][1]) for k in range(4)]
    turned = [
        d[0],
        ((d[1][0] + d[1][1]) * HALF, (d[1][1] - d[1][0]) * HALF),
        (d[2][1], -d[2][0]),
        ((d[3][1] - d[3][0]) * HALF, -(d[3][0] + d[3][1]) * HALF),
    ]
    even, odd = fourths(s), fourths(turned)
    return [even[0], odd[0], even[1], odd[1], even[2], odd[2], even[3], odd[3]]


def near(v):
    return v + 1 - 2 * lax.rem(v, 2)


def far(v):
    return 3 - v


ROUTES = (("x", "near"), ("x", "far"), ("y", "near"), ("y", "far"))
MESH = pl.DeviceIdType.MESH


def hops(offset):
    a, b, d, e = offset
    return min(a, 4 - a) + min(b, 4 - b) + min(e, 8 - e)


FAR_FIRST = sorted(
    ((a, b, d, e) for a in range(4) for b in range(4) for e in range(8) for d in range(2) if (a, b, d, e) != (0, 0, 0, 0)),
    key=lambda o: (-hops(o), (7 * o[0] + 3 * o[1] + 5 * o[3]) % 11),
)


def transform_kernel(
    main_ref, rim_ref, total_ref, counts_hbm, twist_hbm, y_high_hbm, y_low_hbm,
    columns, begin_out,
    counts_ref, twist_y, y_high, y_low, table_sem,
    main0, rim0, main1, rim1, main2, rim2, main3, rim3, main4, rim4,
    tally, inbox, pack, got, waves,
    z_sem, note_send, note_recv, send, recv, py_send, py_recv, wave_send, wave_recv,
):
    x, y, c = (lax.axis_index(a) for a in COORDS)
    j = lax.axis_index("py")
    i = (x * 4 + y) * 2 + c
    me = i * 8 + j
    barrier = pltpu.get_barrier_semaphore()

    def device(x, y, c):
        return {"px_0": x, "px_1": y, "px_2": c}

    tables_in = [
        pltpu.make_async_copy(table, spot, table_sem.at[k])
        for k, (table, spot) in enumerate(
            ((counts_hbm, counts_ref), (twist_hbm, twist_y), (y_high_hbm, y_high), (y_low_hbm, y_low))
        )
    ]
    for copy in tables_in:
        copy.start()
    xs = [x] + [lax.rem(x + k, 4) for k in range(1, 4)]
    ys = [y] + [lax.rem(y + k, 4) for k in range(1, 4)]
    js = [j] + [lax.rem(j + k, 8) for k in range(1, 8)]
    kin = [
        (device(x, y, 1 - c), c == 1),
        (device(x, near(y), c), lax.rem(y, 2) == 1),
        (device(x, far(y), c), y >= 2),
        (device(near(x), y, c), lax.rem(x, 2) == 1),
        (device(far(x), y, c), x >= 2),
    ]
    above, below = {"py": js[1]}, {"py": js[7]}
    for peer in (*(peer for peer, _ in kin), above, below):
        pl.semaphore_signal(barrier, inc=1, device_id=peer, device_id_type=MESH)
    tables_in[0].wait()
    tally[0, 0:1, :] = counts_ref[0, :, 0:TILE].astype(jnp.float32)
    tally[0, 1:2, :] = counts_ref[0, :, TILE:].astype(jnp.float32)
    tally[0, 2:3, :] = jnp.sum(total_ref[...], axis=0, keepdims=True)
    tally[0, 3:8, :] = jnp.zeros((5, TILE), jnp.float32)
    pl.semaphore_wait(barrier, 7)

    def tell(n):
        if n < 3:
            pl.semaphore_signal(z_sem.at[n, 0], inc=1, device_id=above, device_id_type=MESH)
            pl.semaphore_signal(z_sem.at[n, 1], inc=1, device_id=below, device_id_type=MESH)
        copy = pltpu.make_async_remote_copy(
            src_ref=tally.at[n], dst_ref=inbox.at[n], send_sem=note_send.at[n], recv_sem=note_recv.at[n],
            device_id=kin[n][0], device_id_type=MESH,
        )
        copy.start()
        told.append(copy)

    def hear(n):
        if n < 3:
            pl.semaphore_wait(z_sem.at[n, 0], 1)
            pl.semaphore_wait(z_sem.at[n, 1], 1)
        told[n].wait_recv()
        tally[n + 1] = tally[n] + inbox[n]

    sent, told = [], []
    tell(0)

    def remote(src, dst, slot, where):
        copy = pltpu.make_async_remote_copy(
            src_ref=src, dst_ref=dst, send_sem=send.at[slot], recv_sem=recv.at[slot],
            device_id=where, device_id_type=MESH,
        )
        copy.start()
        return copy

    chunks = {}
    for k in (8, 9, *range(8)):
        if k < 8:
            refs = (main_ref.at[k], *(r.at[k] for r in (main0, main1, main2, main3, main4)))
        else:
            refs = (rim_ref.at[k - 8], *(r.at[k - 8] for r in (rim0, rim1, rim2, rim3, rim4)))
        chunks[k] = (*refs, k % 4 if k < 8 else 2 * (k - 8))

    def leg(first, kind):
        v = x if first == "x" else y
        if kind == "near":
            low = lax.rem((v + 1) // 2, 2)
            keep, give = (low, 3 - low), (1 - low, 2 + low)
            partner, other = near(v), far(v)
        else:
            low = 2 * (v // 2)
            keep, give = (low, low + 1), (2 - low, 3 - low)
            partner, other = far(v), near(v)
        if first == "x":
            return keep, give, device(partner, y, c), other, device(other, y, c)
        return keep, give, device(x, partner, c), other, device(x, other, c)

    def core_copy(k, src, b0):
        where = device(x, y, 1 - c)
        if k >= 8:
            parts = [(src.at[:, :, 1 - c], b0)]
        else:
            parts = [(src.at[pl.ds(1 - c + 4 * n, 4), c], b0.at[n]) for n in range(4)]
        for one, two in parts:
            pltpu.make_async_remote_copy(
                src_ref=one, dst_ref=two, send_sem=send.at[7 * k], recv_sem=recv.at[7 * k],
                device_id=where, device_id_type=MESH,
            ).start()

    for k, (src, b0, *_) in chunks.items():
        core_copy(k, src, b0)
    pending = {}

    hear(0)
    tell(1)

    def arrive(k):
        for copy in pending[k]:
            copy.wait_recv()
        sent.extend(pending[k])

    for k, (src, b0, b1, b2, b3, b4, route) in chunks.items():
        pltpu.make_async_copy(b0, b0, recv.at[7 * k]).wait()

        def add0(n, _, src=src, b0=b0, k=k):
            for m in range(4):
                own = src[c + 4 * n + m, 1 - c] if k < 8 else src[n, m, c]
                b0[n, m] = b0[n, m] + own
            return 0

        lax.fori_loop(0, 4, add0, 0)
        first, kind = ROUTES[route]
        _, give, where, _, _ = leg(first, kind)
        pending[k] = []
        for n in range(2):
            block = b0.at[give[n]] if first == "x" else b0.at[:, give[n]]
            pending[k].append(remote(block, b1.at[n], 7 * k + 1 + n, where))

    hear(1)
    tell(2)
    for k, (src, b0, b1, b2, b3, b4, route) in chunks.items():
        arrive(k)
        first, kind = ROUTES[route]
        keep, _, _, other, where = leg(first, kind)
        for n in range(2):
            for m in range(4):
                at = (keep[n], m) if first == "x" else (m, keep[n])
                b0[at] = b0[at] + b1[n, m]
        block = b0.at[other] if first == "x" else b0.at[:, other]
        pending[k] = [remote(block, b2, 7 * k + 3, where)]

    hear(2)
    tell(3)
    for k, (src, b0, b1, b2, b3, b4, route) in chunks.items():
        arrive(k)
        first, kind = ROUTES[route]
        for m in range(4):
            at = (x, m) if first == "x" else (m, y)
            b0[at] = b0[at] + b2[m]
        second = "y" if first == "x" else "x"
        _, give, where, _, _ = leg(second, kind)
        pending[k] = []
        for n in range(2):
            block = b0.at[x, give[n]] if first == "x" else b0.at[give[n], y]
            pending[k].append(remote(block, b3.at[n], 7 * k + 4 + n, where))

    hear(3)
    tell(4)
    for k, (src, b0, b1, b2, b3, b4, route) in chunks.items():
        arrive(k)
        first, kind = ROUTES[route]
        second = "y" if first == "x" else "x"
        keep, _, _, other, where = leg(second, kind)
        for n in range(2):
            at = (x, keep[n]) if first == "x" else (keep[n], y)
            b0[at] = b0[at] + b3[n]
        block = b0.at[x, other] if first == "x" else b0.at[other, y]
        pending[k] = [remote(block, b4, 7 * k + 6, where)]

    hear(4)
    everyone = tally[5]
    amount = jnp.broadcast_to(everyone[2:3, :], (8, TILE))
    spare = lax.broadcasted_iota(jnp.int32, (8, TILE), 0) == 4

    def plane_copy(k, source):
        return pltpu.make_async_remote_copy(
            src_ref=pack.at[k], dst_ref=got.at[source], send_sem=py_send.at[k], recv_sem=py_recv.at[source],
            device_id={"py": k}, device_id_type=MESH,
        )

    edge = []
    for k, (src, b0, b1, b2, b3, b4, route) in chunks.items():
        arrive(k)
        block = b0[x, y] + b4[...]
        if k >= 8:
            edge.append(block)
            if k == 9:
                edge = edge + [pltpu.roll(half, 64, 1) for half in edge] + [jnp.zeros((96, TILE), jnp.float32)]
                turned = jnp.transpose(jnp.concatenate(edge))
                for p in range(PLANES):
                    pack[p, RX:, :] = jnp.where(spare, amount, turned[8 * p : 8 * p + 8, :])
            continue
        pack[k, 0:RX, :] = block

        @pl.when(k != j)
        def _():
            plane_copy(k, j).start()

        @pl.when(k == j)
        def _():
            got[k] = pack[k]

    earlier = jnp.zeros((8, TILE), jnp.float32)
    for n, (_, lower) in enumerate(kin):
        earlier = earlier + jnp.where(lower, inbox[n], 0.0)
    spot = lax.broadcasted_iota(jnp.int32, (8, TILE), 1)
    running = everyone
    for shift in (1, 2, 4, 8, 16, 32, 64):
        running = running + jnp.where(spot >= shift, pltpu.roll(running, shift, 1), 0.0)
    begin = running - everyone + earlier
    whole = jnp.sum(everyone[0:1, :], axis=1, keepdims=True)
    begin_out[0:1, :] = begin[0:1, :]
    begin_out[1:2, :] = begin[1:2, :] + whole
    begin_out[2:8, :] = jnp.zeros((6, TILE), jnp.float32)

    for k in range(1, 8):
        peer = js[k]
        plane_copy(peer, j).wait_send()
        plane_copy(peer, peer).wait_recv()

    for copy in tables_in[1:]:
        copy.wait()
    lane = lax.broadcasted_iota(jnp.int32, (RX, TILE), 1)
    rims = jnp.concatenate([got[s, 32:40, :] for s in range(8)])
    rims = jnp.concatenate([rims, jnp.zeros((64, TILE), jnp.float32)])
    rims = jnp.transpose(rims)[:RX]
    mass_sum = got[0, 36:37, :]
    for s in range(1, 8):
        mass_sum = mass_sum + got[s, 36:37, :]
    inverse = float(PLANES * NX * NY) / jnp.sum(mass_sum, axis=1, keepdims=True)
    blocks = []
    for s in range(8):
        right = pltpu.roll(rims, (-8 * ((s + 7) % 8)) % TILE, 1)
        left = pltpu.roll(rims, (120 - 8 * ((s + 1) % 8)) % TILE, 1)
        value = got[s, 0:32, :] + jnp.where(lane < 4, right, 0.0) + jnp.where(lane >= 125, left, 0.0)
        blocks.append(value * inverse - 1.0)
    turned = []
    for k, (re, im) in enumerate(real_eighths(blocks)):
        tr, ti = twist_y[0, k : k + 1, :], twist_y[1, k : k + 1, :]
        turned.append(jnp.concatenate([re * tr - im * ti, re * ti + im * tr], axis=1))
    high, low = split_bf16(jnp.concatenate(turned))

    def times(a, b):
        return lax.dot_general(a, b, NT, preferred_element_type=jnp.float32)

    wave = times(y_high[...], low) + times(y_low[...], high) + times(y_high[...], high)
    for h in range(2):
        for k in range(TILE):
            waves[2 * k + h] = wave[2 * k : 2 * k + 2, TILE * h : TILE * h + TILE]

    columns[j * 32 + i] = waves[me]

    cs = [c, 1 - c]
    for a, b, d, e in FAR_FIRST:
        pltpu.make_async_remote_copy(
            src_ref=waves.at[((xs[a] * 4 + ys[b]) * 2 + cs[d]) * 8 + js[e]], dst_ref=columns.at[j * 32 + i],
            send_sem=wave_send, recv_sem=wave_recv,
            device_id={"px_0": xs[a], "px_1": ys[b], "px_2": cs[d], "py": js[e]}, device_id_type=MESH,
        ).start()
    for copy in (*sent, *told):
        copy.wait_send()
    for k, (src, b0, *_) in chunks.items():
        pltpu.make_async_copy(b0, b0, send.at[7 * k]).wait()
    others = columns.at[pl.ds(0, DEVICES - 1)]
    pltpu.make_async_copy(others, others, wave_recv).wait()
    pltpu.make_async_copy(others, others, wave_send).wait()


def transform(main, rim, total, counts, wave_tables):
    vmem = pl.BlockSpec(memory_space=pltpu.VMEM)
    f32 = jnp.float32

    def both(*lead):
        return [pltpu.VMEM((PLANES, *lead, RX, TILE), f32), pltpu.VMEM((2, *lead, 8, TILE), f32)]

    dma = pltpu.SemaphoreType.DMA
    return pl.pallas_call(
        transform_kernel,
        out_shape=(
            jax.ShapeDtypeStruct((DEVICES, 2, TILE), f32),
            jax.ShapeDtypeStruct((8, TILE), f32),
        ),
        in_specs=[vmem] * 3 + [pl.BlockSpec(memory_space=pltpu.HBM)] * 4,
        out_specs=(vmem, vmem),
        scratch_shapes=[
            pltpu.VMEM((1, 1, 2 * TILE), jnp.int32),
            pltpu.VMEM((2, 8, TILE), f32),
            pltpu.VMEM((2 * TILE, 2 * TILE), jnp.bfloat16),
            pltpu.VMEM((2 * TILE, 2 * TILE), jnp.bfloat16),
            dma((4,)),
            *both(4, 4), *both(2, 4), *both(4), *both(2), *both(),
            pltpu.VMEM((6, 8, TILE), f32),
            pltpu.VMEM((5, 8, TILE), f32),
            pltpu.VMEM((PLANES, RX + 8, TILE), f32),
            pltpu.VMEM((PLANES, RX + 8, TILE), f32),
            pltpu.VMEM((DEVICES, 2, TILE), f32),
            pltpu.SemaphoreType.REGULAR((3, 2)), dma((5,)), dma((5,)), dma((70,)), dma((70,)), dma((8,)), dma((8,)), dma, dma,
        ],
        compiler_params=pltpu.CompilerParams(
            collective_id=0, has_side_effects=True, vmem_limit_bytes=24 << 20
        ),
        name="transform",
    )(main, rim, total, *(pltpu.with_memory_space_constraint(a, pltpu.HBM) for a in (counts, *wave_tables)))


def finish_kernel(columns, begin_ref, x_both, x_low, twist_x, out_ref, start_ref):
    start_ref[0, :, 0:TILE] = begin_ref[0:1, :].astype(jnp.int32)
    start_ref[0, :, TILE:] = begin_ref[1:2, :].astype(jnp.int32)
    for g in range(4):
        pair = columns[64 * g : 64 * g + 64].reshape(TILE, TILE)
        high, low = split_bf16(jnp.transpose(pair))
        both = jnp.concatenate([high, low], axis=1)
        sums = jnp.dot(both, x_both[...], preferred_element_type=jnp.float32)
        sums = sums + jnp.dot(high, x_low[...], preferred_element_type=jnp.float32)
        parts = [[], []]
        for p in range(2):
            for w in range(4):
                re_sum = im_sum = None
                for q in range(4):
                    rows = slice(32 * w + 8 * q, 32 * w + 8 * q + 8)
                    re = sums[rows, 256 * p : 256 * p + 128]
                    im = sums[rows, 256 * p + 128 : 256 * p + 256]
                    tr, ti = twist_x[0, 8 * q : 8 * q + 8, :], twist_x[1, 8 * q : 8 * q + 8, :]
                    re_part, im_part = re * tr - im * ti, re * ti + im * tr
                    re_sum = re_part if q == 0 else re_sum + re_part
                    im_sum = im_part if q == 0 else im_sum + im_part
                parts[0].append(re_sum)
                parts[1].append(im_sum)
        re, im = (jnp.transpose(jnp.stack(part), (1, 0, 2)) for part in parts)
        for a, value in enumerate(eighths([(re[k], im[k]) for k in range(8)])):
            for n in range(2):
                for p in range(2):
                    out_ref[n, 2 * g + p, :, TILE * a : TILE * a + TILE] = value[n][4 * p : 4 * p + 4]


def finish(columns, begin, wave_tables):
    vmem = pl.BlockSpec(memory_space=pltpu.VMEM)
    return pl.pallas_call(
        finish_kernel,
        out_shape=(
            jax.ShapeDtypeStruct((2, PLANES, 4, NX), jnp.float32),
            jax.ShapeDtypeStruct((1, 1, 2 * TILE), jnp.int32),
        ),
        in_specs=[vmem] * 5,
        out_specs=(vmem, vmem),
        compiler_params=pltpu.CompilerParams(vmem_limit_bytes=24 << 20),
        name="finish",
    )(columns, begin, *wave_tables)


PX = ("px_0", "px_1", "px_2")
PX_PY = ("px_0", "px_1", "px_2", "py")


def local(cell_ids, offset_x, offset_y, mass, live, tile_owner, counts):
    main, rim, total = spread(tile_owner, cell_ids[0], offset_x[0], offset_y[0], mass[0], live[0])
    y_tables, x_tables = tables()
    columns, begin = transform(
        main.reshape(PLANES, BLOCKS // 2, 2, RX, TILE), rim.reshape(2, 4, 4, 2, 8, TILE), total, counts, y_tables
    )
    return finish(columns, begin, x_tables)


def solution(mesh):
    torus = Mesh(mesh.devices.reshape(4, 4, 2, mesh.shape["py"]), ("px_0", "px_1", "px_2", "py"))
    return jax.shard_map(
        local,
        mesh=torus,
        in_specs=(
            P(PX, "py", None),
            P(PX, "py", None),
            P(PX, "py", None),
            P(PX, "py", None),
            P(PX, "py", None),
            P(PX, "py"),
            P(PX, "py", None),
        ),
        out_specs=(P(None, None, PX_PY, None), P(PX, "py", None)),
        check_vma=False,
    )
```

profile of v0, /device:TPU:1, one launch (start us, length us, event | category | flops | bytes accessed | tf_op | source)
XLA Modules:
  0.0 66.1 jit_solution(17173540874181533973)
XLA Ops:
  0.6 0.0 copy-start.2
  0.6 0.0 copy-start.1
  0.7 0.0 copy-start
  0.7 18.7 %spread.1 = (f32[272,32,128]{2,1,0:T(8,128)S(1)}, f32[2,16,2,8,128]{4,3,2,1,0:T(8,128)S(1)}, f32[8,128]{1,0:T(8,128)S(1)}) custom-call(s32[1,640]{1,0:T(1,128)} %owner_hbm.1, s32[640,128]{1,0:T(8,128)} %bitcast.9, bf16[640,128]{1,0:T(8,128)(2,1)} %bitcast.11, bf16[640,128]{1,0:T(8,128)(2,1)} %bitcast.12, bf16[640,128]{1,0:T(8,128)(2,1)} %bitcast.13, ...), custom_call_target="tpu_custom_call" | custom-call | tf_op jit(solution)/shard_map/spread/pallas_call | solution.py:130
  19.3 45.5 %transform.1 = (f32[256,2,128]{2,1,0:T(2,128)S(1)}, f32[8,128]{1,0:T(8,128)S(1)}) custom-call(f32[8,17,2,32,128]{4,3,2,1,0:T(8,128)S(1)} %bitcast.7, f32[2,4,4,2,8,128]{5,4,3,2,1,0:T(8,128)S(1)} %bitcast.8, f32[8,128]{1,0:T(8,128)S(1)} %get-tuple-element.9.total_ref, s32[1,1,256]{2,1,0:T(1,128)} %counts_hbm.1, f32[2,8,128]{2,1,0:T(8,128)} %constant.12.clone.twist_hbm, ...), custom_call_target="tpu_custom_call" | custom-call | tf_op jit(solution)/shard_map/transform/pallas_call | solution.py:545
  64.9 0.0 copy-done.2
  64.9 0.0 copy-done.1
  64.9 0.0 copy-done
  64.9 1.2 %finish.1 = (f32[2,8,4,1024]{3,2,1,0:T(4,128)}, s32[1,1,256]{2,1,0:T(1,128)}) custom-call(f32[256,2,128]{2,1,0:T(2,128)S(1)} %get-tuple-element.10.columns, f32[8,128]{1,0:T(8,128)S(1)} %get-tuple-element.11.begin_ref, bf16[256,512]{1,0:T(8,128)(2,1)S(1)} %copy-done, bf16[128,512]{1,0:T(8,128)(2,1)S(1)} %copy-done.1, f32[2,32,128]{2,1,0:T(8,128)S(1)} %copy-done.2), custom_call_target="tpu_custom_call" | custom-call | tf_op jit(solution)/shard_map/finish/pallas_call | solution.py:606
Async XLA Ops:
  0.6 64.2 %copy-start.2 = (f32[2,32,128]{2,1,0:T(8,128)S(1)}, f32[2,32,128]{2,1,0:T(8,128)}, u32[]{:S(2)}) copy-start(f32[2,32,128]{2,1,0:T(8,128)} %constant.17.clone.twist_x) | copy-start | bytes 98308
  0.6 64.2 %copy-start.1 = (bf16[128,512]{1,0:T(8,128)(2,1)S(1)}, bf16[128,512]{1,0:T(8,128)(2,1)}, u32[]{:S(2)}) copy-start(bf16[128,512]{1,0:T(8,128)(2,1)} %constant.16.clone.x_low) | copy-start | bytes 393220
  0.7 64.2 %copy-start = (bf16[256,512]{1,0:T(8,128)(2,1)S(1)}, bf16[256,512]{1,0:T(8,128)(2,1)}, u32[]{:S(2)}) copy-start(bf16[256,512]{1,0:T(8,128)(2,1)} %constant.15.clone.x_both) | copy-start | bytes 786436
where the time goes:
time: 66.5 us; the launch traced here: 66.1 us
  Pallas kernels  65.4 us (98%)
  between operations  0.69 us (1%)
    pallas_call x1, Pallas kernels, transform(): pl.pallas_call(transform_kernel, out_shape=(jax.ShapeDtypeStruct((DEVICES...  45.5 us
    pallas_call x1, Pallas kernels, spread(): pl.pallas_call(spread_kernel, out_shape=(jax.ShapeDtypeStruct((PLANES * B...  18.7 us

commit v1 on v0

--- a/solution.py
+++ b/solution.py
@@ -65,7 +65,7 @@
         w_s[rows, :] = jnp.where(live_ref[rows, :] == 1, mass_ref[rows, :].astype(jnp.float32), 0.0)
         return 0
 
-    lax.fori_loop(0, tiles // 16, prepare, 0)
+    lax.fori_loop(0, tiles // 16, prepare, 0, unroll=8)
 
     sub = lax.broadcasted_iota(jnp.int32, (8, TILE), 0)
 
@@ -447,26 +447,22 @@
         )
 
     edge = []
-    for k, (src, b0, b1, b2, b3, b4, route) in chunks.items():
+    for k in (8, 9):
         arrive(k)
-        block = b0[x, y] + b4[...]
-        if k >= 8:
-            edge.append(block)
-            if k == 9:
-                edge = edge + [pltpu.roll(half, 64, 1) for half in edge] + [jnp.zeros((96, TILE), jnp.float32)]
-                turned = jnp.transpose(jnp.concatenate(edge))
-                for p in range(PLANES):
-                    pack[p, RX:, :] = jnp.where(spare, amount, turned[8 * p : 8 * p + 8, :])
-            continue
-        pack[k, 0:RX, :] = block
-
-        @pl.when(k != j)
-        def _():
+        edge.append(rim0[k - 8, x, y] + rim4[k - 8])
+    edge = edge + [pltpu.roll(half, 64, 1) for half in edge] + [jnp.zeros((96, TILE), jnp.float32)]
+    turned = jnp.transpose(jnp.concatenate(edge))
+    for p in range(PLANES):
+        pack[p, RX:, :] = jnp.where(spare, amount, turned[8 * p : 8 * p + 8, :])
+    for n in (4, 3, 5, 2, 6, 1, 7, 0):
+        k = js[n]
+        pltpu.make_async_copy(main4.at[k], main4.at[k], recv.at[7 * k + 6]).wait()
+        pack[k, 0:RX, :] = main0[k, x, y] + main4[k]
+        if n:
             plane_copy(k, j).start()
-
-        @pl.when(k == j)
-        def _():
-            got[k] = pack[k]
+    got[j] = pack[j]
+    for k in range(PLANES):
+        sent.extend(pending[k])
 
     earlier = jnp.zeros((8, TILE), jnp.float32)
     for n, (_, lower) in enumerate(kin):

time: 66.5 us -> 65.3 us (0.982)
  Pallas kernels: 65.4 us -> 64.5 us
    pallas_call x1, Pallas kernels: 45.5 us -> 44.8 us  [transform(): pl.pallas_call(transform_kernel, out_shape=(jax.ShapeDtypeStruct((DEVICES...]
where the time goes in v1:
time: 65.3 us; the launch traced here: 65.2 us
  Pallas kernels  64.5 us (99%)
  between operations  0.69 us (1%)
    pallas_call x1, Pallas kernels, transform(): pl.pallas_call(transform_kernel, out_shape=(jax.ShapeDtypeStruct((DEVICES...  44.8 us
    pallas_call x1, Pallas kernels, spread(): pl.pallas_call(spread_kernel, out_shape=(jax.ShapeDtypeStruct((PLANES * B...  18.4 us

profile of v1, /device:TPU:1, one launch (start us, length us, event | category | flops | bytes accessed | tf_op | source)
XLA Modules:
  0.0 65.2 jit_solution(12544851469665414707)
XLA Ops:
  0.6 0.0 copy-start.2
  0.6 0.0 copy-start.1
  0.7 0.0 copy-start
  0.7 18.4 %spread.1 = (f32[272,32,128]{2,1,0:T(8,128)S(1)}, f32[2,16,2,8,128]{4,3,2,1,0:T(8,128)S(1)}, f32[8,128]{1,0:T(8,128)S(1)}) custom-call(s32[1,640]{1,0:T(1,128)} %owner_hbm.1, s32[640,128]{1,0:T(8,128)} %bitcast.9, bf16[640,128]{1,0:T(8,128)(2,1)} %bitcast.11, bf16[640,128]{1,0:T(8,128)(2,1)} %bitcast.12, bf16[640,128]{1,0:T(8,128)(2,1)} %bitcast.13, ...), custom_call_target="tpu_custom_call" | custom-call | tf_op jit(solution)/shard_map/spread/pallas_call | solution.py:130
  19.1 44.8 %transform.1 = (f32[256,2,128]{2,1,0:T(2,128)S(1)}, f32[8,128]{1,0:T(8,128)S(1)}) custom-call(f32[8,17,2,32,128]{4,3,2,1,0:T(8,128)S(1)} %bitcast.7, f32[2,4,4,2,8,128]{5,4,3,2,1,0:T(8,128)S(1)} %bitcast.8, f32[8,128]{1,0:T(8,128)S(1)} %get-tuple-element.9.total_ref, s32[1,1,256]{2,1,0:T(1,128)} %counts_hbm.1, f32[2,8,128]{2,1,0:T(8,128)} %constant.12.clone.twist_hbm, ...), custom_call_target="tpu_custom_call" | custom-call | tf_op jit(solution)/shard_map/transform/pallas_call | solution.py:541
  63.9 0.0 copy-done.2
  63.9 0.0 copy-done.1
  63.9 0.0 copy-done
  63.9 1.2 %finish.1 = (f32[2,8,4,1024]{3,2,1,0:T(4,128)}, s32[1,1,256]{2,1,0:T(1,128)}) custom-call(f32[256,2,128]{2,1,0:T(2,128)S(1)} %get-tuple-element.10.columns, f32[8,128]{1,0:T(8,128)S(1)} %get-tuple-element.11.begin_ref, bf16[256,512]{1,0:T(8,128)(2,1)S(1)} %copy-done, bf16[128,512]{1,0:T(8,128)(2,1)S(1)} %copy-done.1, f32[2,32,128]{2,1,0:T(8,128)S(1)} %copy-done.2), custom_call_target="tpu_custom_call" | custom-call | tf_op jit(solution)/shard_map/finish/pallas_call | solution.py:602
Async XLA Ops:
  0.6 63.3 %copy-start.2 = (f32[2,32,128]{2,1,0:T(8,128)S(1)}, f32[2,32,128]{2,1,0:T(8,128)}, u32[]{:S(2)}) copy-start(f32[2,32,128]{2,1,0:T(8,128)} %constant.17.clone.twist_x) | copy-start | bytes 98308
  0.6 63.3 %copy-start.1 = (bf16[128,512]{1,0:T(8,128)(2,1)S(1)}, bf16[128,512]{1,0:T(8,128)(2,1)}, u32[]{:S(2)}) copy-start(bf16[128,512]{1,0:T(8,128)(2,1)} %constant.16.clone.x_low) | copy-start | bytes 393220
  0.7 63.3 %copy-start = (bf16[256,512]{1,0:T(8,128)(2,1)S(1)}, bf16[256,512]{1,0:T(8,128)(2,1)}, u32[]{:S(2)}) copy-start(bf16[256,512]{1,0:T(8,128)(2,1)} %constant.15.clone.x_both) | copy-start | bytes 786436
